TPU v7x, 32 devices: a whole 2x2x4 slice. The times are simulated.
32 devices in a mesh: sub: 2 (over y), row: 4 (over x, core), col: 4 (over z).
Axes of the slice: x: 2, y: 2, z: 4, core: 2. Of those that a mesh axis runs over, the one named last changes fastest.
Arguments:
- visibility: bfloat16 [2, 16, 512, 4096], P(None, 'sub', 'row', 'col'), may hold values from -13 to 13
- sky_model: bfloat16 [2, 16, 512, 4096], P(None, 'sub', 'row', 'col'), may hold values from -4 to 4, as said below
- antenna_flags: int32 [2, 512], P('sub'), may hold values 0 or 1
- gains_init: float32 [2, 16, 512], P(None, 'sub'), may hold values from -0.5 to 1.5
Outputs:
- gains: float32 [2, 16, 512], P(None, 'sub')
Inputs may be any that keep to these rules, and one draw needn't show every extreme that they name: `sky_model`: model visibility parts lie between -4 and 4.
All inputs are finite; a program needn't handle non-finite values.
Results may differ from a plain program's by a relative error of at most 0.0003.
Values sent between devices are 32-bit elements.
A program may use at most 64 MiB of HBM per device.

v0:
```python
import jax
import jax.numpy as jnp
from jax import lax
from jax.sharding import PartitionSpec as P

TIMES = 8
ITERS = 3


def subband_total(values):
    return lax.psum(values, "sub")


def update_gains(summed, previous):
    denominator = summed[:, 2, :] + 1.0
    quotient = jnp.stack([summed[:, 0, :] / denominator, summed[:, 1, :] / denominator], axis=0)
    updated = 0.5 * (quotient + previous)
    chan_mean = jnp.sum(updated, axis=1) / updated.shape[1]
    overall = subband_total(chan_mean) / lax.axis_size("sub")
    return updated + 0.5 * (overall - chan_mean)[:, None, :]


def time_total(values, selector):
    return jnp.einsum(
        "crk,kq->crq",
        values,
        selector,
        precision=lax.Precision.HIGHEST,
        preferred_element_type=jnp.float32,
    )


def contract(matrix, vector):
    return jnp.einsum("cpq,cq->cp", matrix, vector, precision=lax.Precision.HIGHEST)


def body(visibility, sky_model, antenna_flags, gains_init):
    block_rows = visibility.shape[2]
    wide_cols = visibility.shape[3]
    block_cols = wide_cols // TIMES
    row_at = lax.axis_index("row") * block_rows
    col_at = lax.axis_index("col") * block_cols
    flag_value = antenna_flags[0].astype(jnp.float32)
    row_flag = lax.dynamic_slice_in_dim(flag_value, row_at, block_rows)
    col_flag = lax.dynamic_slice_in_dim(flag_value, col_at, block_cols)
    row_ids = row_at + lax.iota(jnp.int32, block_rows)
    col_ids = col_at + lax.iota(jnp.int32, block_cols)
    weight = (
        row_flag[:, None]
        * col_flag[None, :]
        * (row_ids[:, None] != col_ids[None, :]).astype(jnp.float32)
    )
    selector = (
        lax.iota(jnp.int32, wide_cols)[:, None] // TIMES == lax.iota(jnp.int32, block_cols)[None, :]
    ).astype(jnp.float32)
    vis_re = visibility[0].astype(jnp.float32)
    vis_im = visibility[1].astype(jnp.float32)
    mod_re = sky_model[0].astype(jnp.float32)
    mod_im = sky_model[1].astype(jnp.float32)
    cross_re = time_total(vis_re * mod_re + vis_im * mod_im, selector) * weight
    cross_im = time_total(vis_im * mod_re - vis_re * mod_im, selector) * weight
    power_sum = time_total(mod_re * mod_re + mod_im * mod_im, selector) * weight
    gain_values = gains_init
    for step_index in range(ITERS):
        col_gains = lax.dynamic_slice_in_dim(gain_values, col_at, block_cols, 2)
        gain_re = col_gains[0]
        gain_im = col_gains[1]
        num_re = contract(cross_re, gain_re) - contract(cross_im, gain_im)
        num_im = contract(cross_re, gain_im) + contract(cross_im, gain_re)
        denominator = contract(power_sum, gain_re * gain_re + gain_im * gain_im)
        partial_value = jnp.stack([num_re, num_im, denominator], axis=1)
        summed = lax.psum(partial_value, "col")
        previous = lax.dynamic_slice_in_dim(gain_values, row_at, block_rows, 2)
        gain_block = update_gains(summed, previous)
        gain_values = lax.all_gather(gain_block, "row", axis=2, tiled=True)
    return gain_values


def solution(mesh):
    return jax.shard_map(
        body,
        mesh=mesh,
        in_specs=(
            P(None, "sub", "row", "col"),
            P(None, "sub", "row", "col"),
            P("sub", None),
            P(None, "sub", None),
        ),
        out_specs=P(None, "sub", None),
        check_vma=False,
    )
```

profile of v0, /device:TPU:0, one launch (start us, length us, event | category | flops | bytes accessed | tf_op | source)
XLA Modules:
  0.0 111.2 jit_solution(4182115625880762958)
XLA Ops:
  0.0 0.7 convert_element_type.26
  0.7 0.7 fusion.51
  1.4 0.1 multiply_select_fusion
  1.5 0.0 copy-start.1
  1.5 0.0 copy-start.2
  1.5 6.6 %fusion.25 = f32[8,128,128]{2,1,0:T(8,128)S(1)} fusion(bf16[2,8,128,1024]{3,2,1,0:T(8,128)(2,1)} %param.4, bf16[2,8,128,1024]{3,2,1,0:T(8,128)(2,1)} %param.5, f32[128,128]{1,0:T(8,128)S(1)} %multiply_select_fusion, s32[1024]{0:T(1024)S(1)} %add_select_fusion), kind=kOutput, calls=%fused_computation.26 | convolution fusion | flops 1618214912 | bytes 8982528 | tf_op jit(solution)/shard_map/crk,kq->crq/dot_general | solution.py:24
  8.1 0.9 fusion.61
  9.0 0.9 fusion.59
  9.9 0.0 copy-done.1
  10.0 0.0 copy-done.2
  10.0 3.0 %fusion.28 = f32[8,128,128]{2,1,0:T(8,128)S(1)} fusion(bf16[2,8,128,1024]{3,2,1,0:T(8,128)(2,1)S(1)} %copy-done.1, bf16[2,8,128,1024]{3,2,1,0:T(8,128)(2,1)S(1)} %copy-done.2, f32[128,128]{1,0:T(8,128)S(1)} %multiply_select_fusion, s32[1024]{0:T(1024)S(1)} %add_select_fusion), kind=kOutput, calls=%fused_computation.27 | convolution fusion | flops 1618214912 | bytes 8982528 | tf_op jit(solution)/shard_map/crk,kq->crq/dot_general | solution.py:24
  12.9 0.9 fusion.60
  13.9 0.0 copy-start
  13.9 0.9 fusion.58
  14.8 2.7 %fusion.22 = f32[8,128,128]{2,1,0:T(8,128)S(1)} fusion(bf16[2,8,128,1024]{3,2,1,0:T(8,128)(2,1)S(1)} %copy-done.2, f32[128,128]{1,0:T(8,128)S(1)} %multiply_select_fusion, s32[1024]{0:T(1024)S(1)} %add_select_fusion), kind=kOutput, calls=%fused_computation.25 | convolution fusion | flops 1616117760 | bytes 4788224 | tf_op jit(solution)/shard_map/crk,kq->crq/dot_general | solution.py:24
  17.5 0.9 fusion.62
  18.4 20.4 %psum.42 = f32[8,3,128]{2,0,1:T(8,128)S(1)} all-reduce(f32[8,3,128]{2,0,1:T(8,128)S(1)} %pad_maximum_fusion), channel_id=1, replica_groups=mesh['sub'=2,'row'=4,'col'=4] {'col'}, use_global_device_ids=true, to_apply=%region_0.1 | all-reduce | flops 3072 | bytes 24576 | tf_op jit(solution)/shard_map/psum | solution.py:72
  38.9 0.0 copy-done
  38.9 4.9 %psum.43 = f32[2,128]{1,0:T(2,128)S(1)} all-reduce(f32[2,128]{1,0:T(2,128)S(1)} %broadcast_multiply_fusion.2), channel_id=1, replica_groups=mesh['sub'=2,'row'=4,'col'=4] {'sub'}, use_global_device_ids=true, to_apply=%region_2.3 | all-reduce | flops 256 | bytes 2048 | tf_op jit(solution)/shard_map/psum | solution.py:11
  43.9 5.2 %all_gather.9 = f32[2,8,512]{2,1,0:T(8,128)S(1)} all-gather(f32[2,8,128]{2,1,0:T(8,128)S(1)} %broadcast_add_fusion.2), channel_id=1, replica_groups=mesh['sub'=2,'row'=4,'col'=4] {'row'}, dimensions={2}, use_global_device_ids=true | all-gather | bytes 40960 | tf_op jit(solution)/shard_map/all_gather | solution.py:75
  49.1 0.9 fusion.67
  50.0 0.9 fusion.66
  50.9 0.9 fusion.63
  51.8 0.9 fusion.65
  52.8 0.9 fusion.64
  53.7 15.5 %psum.44 = f32[8,3,128]{2,0,1:T(8,128)S(1)} all-reduce(f32[8,3,128]{2,0,1:T(8,128)S(1)} %pad_maximum_fusion.1), channel_id=1, replica_groups=mesh['sub'=2,'row'=4,'col'=4] {'col'}, use_global_device_ids=true, to_apply=%region_3.4 | all-reduce | flops 3072 | bytes 24576 | tf_op jit(solution)/shard_map/psum | solution.py:72
  69.3 4.9 %psum.45 = f32[2,128]{1,0:T(2,128)S(1)} all-reduce(f32[2,128]{1,0:T(2,128)S(1)} %broadcast_multiply_fusion.1), channel_id=1, replica_groups=mesh['sub'=2,'row'=4,'col'=4] {'sub'}, use_global_device_ids=true, to_apply=%region_5.6 | all-reduce | flops 256 | bytes 2048 | tf_op jit(solution)/shard_map/psum | solution.py:11
  74.3 5.2 %all_gather.10 = f32[2,8,512]{2,1,0:T(8,128)S(1)} all-gather(f32[2,8,128]{2,1,0:T(8,128)S(1)} %broadcast_add_fusion.1), channel_id=1, replica_groups=mesh['sub'=2,'row'=4,'col'=4] {'row'}, dimensions={2}, use_global_device_ids=true | all-gather | bytes 40960 | tf_op jit(solution)/shard_map/all_gather | solution.py:75
  79.5 0.9 fusion.72
  80.4 0.9 fusion.71
  81.3 0.9 fusion.69
  82.2 0.9 fusion.70
  83.2 0.9 fusion.68
  84.1 16.2 %psum.46 = f32[8,3,128]{2,0,1:T(8,128)S(1)} all-reduce(f32[8,3,128]{2,0,1:T(8,128)S(1)} %pad_maximum_fusion.2), channel_id=1, replica_groups=mesh['sub'=2,'row'=4,'col'=4] {'col'}, use_global_device_ids=true, to_apply=%region_6.7 | all-reduce | flops 3072 | bytes 24576 | tf_op jit(solution)/shard_map/psum | solution.py:72
  100.4 4.9 %psum.47 = f32[2,128]{1,0:T(2,128)S(1)} all-reduce(f32[2,128]{1,0:T(2,128)S(1)} %broadcast_multiply_fusion), channel_id=1, replica_groups=mesh['sub'=2,'row'=4,'col'=4] {'sub'}, use_global_device_ids=true, to_apply=%region_8.9 | all-reduce | flops 256 | bytes 2048 | tf_op jit(solution)/shard_map/psum | solution.py:11
  105.3 5.2 %all_gather.11 = f32[2,8,512]{2,1,0:T(8,128)S(1)} all-gather(f32[2,8,128]{2,1,0:T(8,128)S(1)} %broadcast_add_fusion), channel_id=1, replica_groups=mesh['sub'=2,'row'=4,'col'=4] {'row'}, dimensions={2}, use_global_device_ids=true | all-gather | bytes 40960 | tf_op jit(solution)/shard_map/all_gather | solution.py:75
  110.5 0.6 copy.30
  (29 shorter events, 0.3 us)
Async XLA Ops:
  1.5 8.4 %copy-start.1 = (bf16[2,8,128,1024]{3,2,1,0:T(8,128)(2,1)S(1)}, bf16[2,8,128,1024]{3,2,1,0:T(8,128)(2,1)}, u32[]{:S(2)}) copy-start(bf16[2,8,128,1024]{3,2,1,0:T(8,128)(2,1)} %param.4) | copy-start | bytes 12582916
  1.5 8.4 %copy-start.2 = (bf16[2,8,128,1024]{3,2,1,0:T(8,128)(2,1)S(1)}, bf16[2,8,128,1024]{3,2,1,0:T(8,128)(2,1)}, u32[]{:S(2)}) copy-start(bf16[2,8,128,1024]{3,2,1,0:T(8,128)(2,1)} %param.5) | copy-start | bytes 12582916
  13.9 25.0 %copy-start = (f32[2,8,512]{2,1,0:T(8,128)S(1)}, f32[2,8,512]{2,1,0:T(8,128)}, u32[]{:S(2)}) copy-start(f32[2,8,512]{2,1,0:T(8,128)} %param.7) | copy-start | bytes 98308
where the time goes:
time: 112 us; the launch traced here: 111 us
  blocking collectives  82.5 us (74%)
  matrix products  26.1 us (23%)
  other arithmetic  1.73 us (2%)
    psum x3, blocking collectives, body(): summed = lax.psum(partial_value, 'col')  52.2 us
    all_gather x3, blocking collectives, body(): gain_values = lax.all_gather(gain_block, 'row', axis=2, tiled=True)  15.6 us
    psum x3, blocking collectives, subband_total(): return lax.psum(values, 'sub')  14.8 us
    dot_general x15, matrix products, contract(): jnp.einsum('cpq,cq->cp', matrix, vector, precision=lax.Precision.HIGHEST)  13.9 us
    dot_general x3, matrix products, time_total(): jnp.einsum('crk,kq->crq', values, selector, precision=lax.Precision.HIGHE...  12.3 us

commit v1 on v0

--- a/solution.py
+++ b/solution.py
@@ -72,7 +72,14 @@
         summed = lax.psum(partial_value, "col")
         previous = lax.dynamic_slice_in_dim(gain_values, row_at, block_rows, 2)
         gain_block = update_gains(summed, previous)
-        gain_values = lax.all_gather(gain_block, "row", axis=2, tiled=True)
+        ring = [gain_block]
+        for hop in range(3):
+            ring.append(lax.ppermute(ring[-1], "row", [(dev, (dev + 1) % 4) for dev in range(4)]))
+        gain_values = jnp.roll(
+            jnp.concatenate(ring[::-1], axis=2),
+            (lax.axis_index("row") + 1) * ring[0].shape[2],
+            axis=2,
+        )
     return gain_values
 
 

time: 112 us -> 126 us (1.12)
  waiting for transfers between devices: 0 us -> 27.7 us
  blocking collectives: 82.5 us -> 67 us
  matrix products: 26.1 us -> 28.3 us
    ppermute x0 -> x9, waiting for transfers between devices: none -> 27.7 us  [body(): lax.ppermute(ring[-1], 'row', [(dev, (dev + 1) % 4) for dev in range(4)])]
    all_gather x3 -> x0, blocking collectives: 15.6 us -> none  [body(): gain_values = lax.all_gather(gain_block, 'row', axis=2, tiled=True)]
    dot_general x3, matrix products: 12.3 us -> 14.5 us  [time_total(): jnp.einsum('crk,kq->crq', values, selector, precision=lax.Precision.HIGHE...]
  transfers between devices with their start and end apart: 0 -> 9, of which waited for: 0 -> 9; matrix products, arithmetic and copies ran while one was open for 0% -> 0% of each run, Pallas kernels for 0% -> 0%
where the time goes in v1:
time: 126 us
  blocking collectives  67 us (53%)
  matrix products  28.3 us (22%)
  waiting for transfers between devices  27.7 us (22%)
  other arithmetic  2.13 us (2%)
    psum x3, blocking collectives, body(): summed = lax.psum(partial_value, 'col')  52.2 us
    ppermute x9, waiting for transfers between devices, body(): lax.ppermute(ring[-1], 'row', [(dev, (dev + 1) % 4) for dev in range(4)])  27.7 us
    psum x3, blocking collectives, subband_total(): return lax.psum(values, 'sub')  14.8 us
    dot_general x3, matrix products, time_total(): jnp.einsum('crk,kq->crq', values, selector, precision=lax.Precision.HIGHE...  14.5 us
    dot_general x15, matrix products, contract(): jnp.einsum('cpq,cq->cp', matrix, vector, precision=lax.Precision.HIGHEST)  13.9 us
  transfers between devices with their start and end apart: 9, of which 9 were waited for; matrix products, arithmetic and copies ran while one was open for 0% of the time, Pallas kernels for 0%

profile of v1, /device:TPU:0, one launch (start us, length us, event | category | flops | bytes accessed | tf_op | source)
XLA Modules:
  0.0 125.6 jit_solution(2977251343283844320)
XLA Ops:
  0.0 0.7 convert_element_type.26
  0.7 0.1 multiply_select_fusion
  0.8 0.0 copy-start.1
  0.8 0.0 copy-start.2
  0.8 6.6 %fusion.25 = f32[8,128,128]{2,1,0:T(8,128)S(1)} fusion(bf16[2,8,128,1024]{3,2,1,0:T(8,128)(2,1)} %param.6, bf16[2,8,128,1024]{3,2,1,0:T(8,128)(2,1)} %param.7, f32[128,128]{1,0:T(8,128)S(1)} %multiply_select_fusion, s32[1024]{0:T(1024)S(1)} %add_select_fusion), kind=kOutput, calls=%fused_computation.26 | convolution fusion | flops 1618214912 | bytes 8982528 | tf_op jit(solution)/shard_map/crk,kq->crq/dot_general | solution.py:24
  7.4 0.0 copy-start
  7.4 3.0 %fusion.28 = f32[8,128,128]{2,1,0:T(8,128)S(1)} fusion(bf16[2,8,128,1024]{3,2,1,0:T(8,128)(2,1)S(1)} %copy-done.1, bf16[2,8,128,1024]{3,2,1,0:T(8,128)(2,1)S(1)} %copy-done.2, f32[128,128]{1,0:T(8,128)S(1)} %multiply_select_fusion, s32[1024]{0:T(1024)S(1)} %add_select_fusion), kind=kOutput, calls=%fused_computation.27 | convolution fusion | flops 1618214912 | bytes 8982528 | tf_op jit(solution)/shard_map/crk,kq->crq/dot_general | solution.py:24
  10.4 0.9 fusion.68
  11.3 0.9 fusion.66
  12.3 0.9 fusion.67
  13.2 0.9 fusion.65
  14.1 4.9 %fusion.22 = f32[8,128,128]{2,1,0:T(8,128)S(1)} fusion(bf16[2,8,128,1024]{3,2,1,0:T(8,128)(2,1)} %param.7, f32[128,128]{1,0:T(8,128)S(1)} %multiply_select_fusion, s32[1024]{0:T(1024)S(1)} %add_select_fusion), kind=kOutput, calls=%fused_computation.25 | convolution fusion | flops 1616117760 | bytes 4788224 | tf_op jit(solution)/shard_map/crk,kq->crq/dot_general | solution.py:24
  19.1 0.9 fusion.69
  20.0 20.4 %psum.42 = f32[8,3,128]{2,0,1:T(8,128)S(1)} all-reduce(f32[8,3,128]{2,0,1:T(8,128)S(1)} %pad_maximum_fusion), channel_id=1, replica_groups=mesh['sub'=2,'row'=4,'col'=4] {'col'}, use_global_device_ids=true, to_apply=%region_0.1 | all-reduce | flops 3072 | bytes 24576 | tf_op jit(solution)/shard_map/psum | solution.py:72
  40.5 4.9 %psum.43 = f32[2,128]{1,0:T(2,128)S(1)} all-reduce(f32[2,128]{1,0:T(2,128)S(1)} %broadcast_multiply_fusion.2), channel_id=1, replica_groups=mesh['sub'=2,'row'=4,'col'=4] {'sub'}, use_global_device_ids=true, to_apply=%region_2.3 | all-reduce | flops 256 | bytes 2048 | tf_op jit(solution)/shard_map/psum | solution.py:11
  45.5 0.2 collective-permute-start
  45.7 3.1 %collective-permute-done = f32[2,8,128]{2,1,0:T(8,128)S(1)} collective-permute-done((f32[2,8,128]{2,1,0:T(8,128)S(1)}, f32[2,8,128]{2,1,0:T(8,128)S(1)}, u32[]{:S(2)}, u32[]{:S(2)}) %collective-permute-start) | collective-permute-done | bytes 8224 | tf_op jit(solution)/shard_map/ppermute | solution.py:77
  48.8 3.1 %collective-permute-done.1 = f32[2,8,128]{2,1,0:T(8,128)S(1)} collective-permute-done((f32[2,8,128]{2,1,0:T(8,128)S(1)}, f32[2,8,128]{2,1,0:T(8,128)S(1)}, u32[]{:S(2)}, u32[]{:S(2)}) %collective-permute-start.1) | collective-permute-done | bytes 8224 | tf_op jit(solution)/shard_map/ppermute | solution.py:77
  51.9 3.1 %collective-permute-done.2 = f32[2,8,128]{2,1,0:T(8,128)S(1)} collective-permute-done((f32[2,8,128]{2,1,0:T(8,128)S(1)}, f32[2,8,128]{2,1,0:T(8,128)S(1)}, u32[]{:S(2)}, u32[]{:S(2)}) %collective-permute-start.2) | collective-permute-done | bytes 8224 | tf_op jit(solution)/shard_map/ppermute | solution.py:77
  54.9 0.1 fusion.57
  55.0 0.9 fusion.73
  55.9 0.9 fusion.70
  56.9 0.9 fusion.72
  57.8 0.9 fusion.71
  58.7 0.9 fusion.74
  59.7 15.5 %psum.44 = f32[8,3,128]{2,0,1:T(8,128)S(1)} all-reduce(f32[8,3,128]{2,0,1:T(8,128)S(1)} %pad_maximum_fusion.1), channel_id=1, replica_groups=mesh['sub'=2,'row'=4,'col'=4] {'col'}, use_global_device_ids=true, to_apply=%region_3.5 | all-reduce | flops 3072 | bytes 24576 | tf_op jit(solution)/shard_map/psum | solution.py:72
  75.2 0.1 fusion.61
  75.3 4.9 %psum.45 = f32[2,128]{1,0:T(2,128)S(1)} all-reduce(f32[2,128]{1,0:T(2,128)S(1)} %broadcast_multiply_fusion.1), channel_id=1, replica_groups=mesh['sub'=2,'row'=4,'col'=4] {'sub'}, use_global_device_ids=true, to_apply=%region_5.7 | all-reduce | flops 256 | bytes 2048 | tf_op jit(solution)/shard_map/psum | solution.py:11
  80.3 0.1 broadcast_add_fusion.1
  80.3 0.0 collective-permute-start.3
  80.4 3.1 %collective-permute-done.3 = f32[2,8,128]{2,1,0:T(8,128)S(1)} collective-permute-done((f32[2,8,128]{2,1,0:T(8,128)S(1)}, f32[2,8,128]{2,1,0:T(8,128)S(1)}, u32[]{:S(2)}, u32[]{:S(2)}) %collective-permute-start.3) | collective-permute-done | bytes 8224 | tf_op jit(solution)/shard_map/ppermute | solution.py:77
  83.4 0.0 collective-permute-start.4
  83.4 3.1 %collective-permute-done.4 = f32[2,8,128]{2,1,0:T(8,128)S(1)} collective-permute-done((f32[2,8,128]{2,1,0:T(8,128)S(1)}, f32[2,8,128]{2,1,0:T(8,128)S(1)}, u32[]{:S(2)}, u32[]{:S(2)}) %collective-permute-start.4) | collective-permute-done | bytes 8224 | tf_op jit(solution)/shard_map/ppermute | solution.py:77
  86.5 3.1 %collective-permute-done.5 = f32[2,8,128]{2,1,0:T(8,128)S(1)} collective-permute-done((f32[2,8,128]{2,1,0:T(8,128)S(1)}, f32[2,8,128]{2,1,0:T(8,128)S(1)}, u32[]{:S(2)}, u32[]{:S(2)}) %collective-permute-start.5) | collective-permute-done | bytes 8224 | tf_op jit(solution)/shard_map/ppermute | solution.py:77
  89.6 0.1 fusion.56
  89.7 0.9 fusion.76
  90.6 0.9 fusion.77
  91.5 0.9 fusion.78
  92.4 0.9 fusion.75
  93.4 0.9 fusion.79
  94.3 16.2 %psum.46 = f32[8,3,128]{2,0,1:T(8,128)S(1)} all-reduce(f32[8,3,128]{2,0,1:T(8,128)S(1)} %pad_maximum_fusion.2), channel_id=1, replica_groups=mesh['sub'=2,'row'=4,'col'=4] {'col'}, use_global_device_ids=true, to_apply=%region_6.8 | all-reduce | flops 3072 | bytes 24576 | tf_op jit(solution)/shard_map/psum | solution.py:72
  110.6 0.1 fusion.60
  110.7 4.9 %psum.47 = f32[2,128]{1,0:T(2,128)S(1)} all-reduce(f32[2,128]{1,0:T(2,128)S(1)} %broadcast_multiply_fusion), channel_id=1, replica_groups=mesh['sub'=2,'row'=4,'col'=4] {'sub'}, use_global_device_ids=true, to_apply=%region_8.10 | all-reduce | flops 256 | bytes 2048 | tf_op jit(solution)/shard_map/psum | solution.py:11
  115.6 0.1 broadcast_add_fusion
  115.7 3.1 %collective-permute-done.6 = f32[2,8,128]{2,1,0:T(8,128)S(1)} collective-permute-done((f32[2,8,128]{2,1,0:T(8,128)S(1)}, f32[2,8,128]{2,1,0:T(8,128)S(1)}, u32[]{:S(2)}, u32[]{:S(2)}) %collective-permute-start.6) | collective-permute-done | bytes 8224 | tf_op jit(solution)/shard_map/ppermute | solution.py:77
  118.8 3.1 %collective-permute-done.7 = f32[2,8,128]{2,1,0:T(8,128)S(1)} collective-permute-done((f32[2,8,128]{2,1,0:T(8,128)S(1)}, f32[2,8,128]{2,1,0:T(8,128)S(1)}, u32[]{:S(2)}, u32[]{:S(2)}) %collective-permute-start.7) | collective-permute-done | bytes 8224 | tf_op jit(solution)/shard_map/ppermute | solution.py:77
  121.8 3.1 %collective-permute-done.8 = f32[2,8,128]{2,1,0:T(8,128)S(1)} collective-permute-done((f32[2,8,128]{2,1,0:T(8,128)S(1)}, f32[2,8,128]{2,1,0:T(8,128)S(1)}, u32[]{:S(2)}, u32[]{:S(2)}) %collective-permute-start.8) | collective-permute-done | bytes 8224 | tf_op jit(solution)/shard_map/ppermute | solution.py:77
  124.9 0.6 fusion.41
  (35 shorter events, 0.2 us)
Async XLA Ops:
  0.8 6.6 %copy-start.1 = (bf16[2,8,128,1024]{3,2,1,0:T(8,128)(2,1)S(1)}, bf16[2,8,128,1024]{3,2,1,0:T(8,128)(2,1)}, u32[]{:S(2)}) copy-start(bf16[2,8,128,1024]{3,2,1,0:T(8,128)(2,1)} %param.6) | copy-start | bytes 12582916
  0.8 6.6 %copy-start.2 = (bf16[2,8,128,1024]{3,2,1,0:T(8,128)(2,1)S(1)}, bf16[2,8,128,1024]{3,2,1,0:T(8,128)(2,1)}, u32[]{:S(2)}) copy-start(bf16[2,8,128,1024]{3,2,1,0:T(8,128)(2,1)} %param.7) | copy-start | bytes 12582916
  7.4 3.0 %copy-start = (f32[2,8,512]{2,1,0:T(8,128)S(1)}, f32[2,8,512]{2,1,0:T(8,128)}, u32[]{:S(2)}) copy-start(f32[2,8,512]{2,1,0:T(8,128)} %param.9) | copy-start | bytes 98308
  45.5 3.3 %collective-permute-start = (f32[2,8,128]{2,1,0:T(8,128)S(1)}, f32[2,8,128]{2,1,0:T(8,128)S(1)}, u32[]{:S(2)}, u32[]{:S(2)}) collective-permute-start(f32[2,8,128]{2,1,0:T(8,128)S(1)} %broadcast_add_fusion.2), channel_id=1, source_target_pairs={{0,4},{4,8},{8,12},{12,0},{1,5},{5,9},{9,13},{13,1},{2,6},{6,10},{... | collective-permute-start | bytes 24584 | tf_op jit(solution)/shard_map/ppermute | solution.py:77
  48.8 3.1 %collective-permute-start.1 = (f32[2,8,128]{2,1,0:T(8,128)S(1)}, f32[2,8,128]{2,1,0:T(8,128)S(1)}, u32[]{:S(2)}, u32[]{:S(2)}) collective-permute-start(f32[2,8,128]{2,1,0:T(8,128)S(1)} %collective-permute-done), channel_id=1, source_target_pairs={{0,4},{4,8},{8,12},{12,0},{1,5},{5,9},{9,13},{13,1},{2,6},{6,10},{... | collective-permute-start | bytes 24584 | tf_op jit(solution)/shard_map/ppermute | solution.py:77
  51.9 3.1 %collective-permute-start.2 = (f32[2,8,128]{2,1,0:T(8,128)S(1)}, f32[2,8,128]{2,1,0:T(8,128)S(1)}, u32[]{:S(2)}, u32[]{:S(2)}) collective-permute-start(f32[2,8,128]{2,1,0:T(8,128)S(1)} %collective-permute-done.1), channel_id=1, source_target_pairs={{0,4},{4,8},{8,12},{12,0},{1,5},{5,9},{9,13},{13,1},{2,6},{6,10},{... | collective-permute-start | bytes 24584 | tf_op jit(solution)/shard_map/ppermute | solution.py:77
  80.3 3.1 %collective-permute-start.3 = (f32[2,8,128]{2,1,0:T(8,128)S(1)}, f32[2,8,128]{2,1,0:T(8,128)S(1)}, u32[]{:S(2)}, u32[]{:S(2)}) collective-permute-start(f32[2,8,128]{2,1,0:T(8,128)S(1)} %broadcast_add_fusion.1), channel_id=1, source_target_pairs={{0,4},{4,8},{8,12},{12,0},{1,5},{5,9},{9,13},{13,1},{2,6},{6,10},{... | collective-permute-start | bytes 24584 | tf_op jit(solution)/shard_map/ppermute | solution.py:77
  83.4 3.1 %collective-permute-start.4 = (f32[2,8,128]{2,1,0:T(8,128)S(1)}, f32[2,8,128]{2,1,0:T(8,128)S(1)}, u32[]{:S(2)}, u32[]{:S(2)}) collective-permute-start(f32[2,8,128]{2,1,0:T(8,128)S(1)} %collective-permute-done.3), channel_id=1, source_target_pairs={{0,4},{4,8},{8,12},{12,0},{1,5},{5,9},{9,13},{13,1},{2,6},{6,10},{... | collective-permute-start | bytes 24584 | tf_op jit(solution)/shard_map/ppermute | solution.py:77
  86.5 3.1 %collective-permute-start.5 = (f32[2,8,128]{2,1,0:T(8,128)S(1)}, f32[2,8,128]{2,1,0:T(8,128)S(1)}, u32[]{:S(2)}, u32[]{:S(2)}) collective-permute-start(f32[2,8,128]{2,1,0:T(8,128)S(1)} %collective-permute-done.4), channel_id=1, source_target_pairs={{0,4},{4,8},{8,12},{12,0},{1,5},{5,9},{9,13},{13,1},{2,6},{6,10},{... | collective-permute-start | bytes 24584 | tf_op jit(solution)/shard_map/ppermute | solution.py:77
  115.7 3.1 %collective-permute-start.6 = (f32[2,8,128]{2,1,0:T(8,128)S(1)}, f32[2,8,128]{2,1,0:T(8,128)S(1)}, u32[]{:S(2)}, u32[]{:S(2)}) collective-permute-start(f32[2,8,128]{2,1,0:T(8,128)S(1)} %broadcast_add_fusion), channel_id=1, source_target_pairs={{0,4},{4,8},{8,12},{12,0},{1,5},{5,9},{9,13},{13,1},{2,6},{6,10},{... | collective-permute-start | bytes 24584 | tf_op jit(solution)/shard_map/ppermute | solution.py:77
  118.8 3.1 %collective-permute-start.7 = (f32[2,8,128]{2,1,0:T(8,128)S(1)}, f32[2,8,128]{2,1,0:T(8,128)S(1)}, u32[]{:S(2)}, u32[]{:S(2)}) collective-permute-start(f32[2,8,128]{2,1,0:T(8,128)S(1)} %collective-permute-done.6), channel_id=1, source_target_pairs={{0,4},{4,8},{8,12},{12,0},{1,5},{5,9},{9,13},{13,1},{2,6},{6,10},{... | collective-permute-start | bytes 24584 | tf_op jit(solution)/shard_map/ppermute | solution.py:77
  121.8 3.1 %collective-permute-start.8 = (f32[2,8,128]{2,1,0:T(8,128)S(1)}, f32[2,8,128]{2,1,0:T(8,128)S(1)}, u32[]{:S(2)}, u32[]{:S(2)}) collective-permute-start(f32[2,8,128]{2,1,0:T(8,128)S(1)} %collective-permute-done.7), channel_id=1, source_target_pairs={{0,4},{4,8},{8,12},{12,0},{1,5},{5,9},{9,13},{13,1},{2,6},{6,10},{... | collective-permute-start | bytes 24584 | tf_op jit(solution)/shard_map/ppermute | solution.py:77
